TPU v7x, 512 devices: a whole 4x4x16 slice. The times are simulated.
512 devices in a mesh: rep: 4 (over x_hi, core), row: 32 (over x_lo, z), col: 4 (over y).
Axes of the slice: x: 4 (x_hi: 2, x_lo: 2; x = x_hi * 2 + x_lo), y: 4, z: 16, core: 2. Of those that a mesh axis runs over, the one named last changes fastest.
Arguments:
- spin_init: bfloat16 [256, 8192], P('rep', 'row'), may hold values from -1 to 1, as said below
- couplings: bfloat16 [32, 4, 64, 8192], P(None, 'col', None, 'row'), may hold values from -1 to 1, as said below
- flip_noise: float32 [10, 256, 8192], P(None, 'rep', 'row'), may hold values from 0 to 17, as said below
- colors: int32 [8192], P('row'), may hold values 0 or 1
- beta_steps: int32 [256], replicated, may hold values from 96 to 1024
- partners: int32 [256], replicated, may hold values from 0 to 255, as said below
- swap_noise: float32 [256], replicated, may hold values from 0 to 17, as said below
Outputs:
- spins_out: bfloat16 [256, 8192], P('rep', 'row')
- energies: float32 [256], P('rep')
Inputs may be any that keep to these rules, and one draw needn't show every extreme that they name: `spin_init`: every entry is -1 or +1. `couplings`: the 8192 x 8192 matrix is symmetric, zero on its diagonal, and every other entry is -1 or +1. `flip_noise`: independent exponential variates of mean one. `swap_noise`: independent exponential variates of mean one. Pairs slots: partners[partners[r]] = r and partners[r] != r for every slot.
All inputs are finite; a program needn't handle non-finite values. No bound on the sum of `colors` on one device may be relied on, other than what follows from the above.
Results may differ from a plain program's by a relative error of at most 0.001.
Values may be sent and summed in bfloat16 or wider, within the bound.
No kernel may reach another device: no remote copies, remote signals or barrier semaphores. Data moves between devices by JAX's collectives and lax.ppermute only.
A program may use at most 64 MiB of HBM per device.

v0:
```python
import math

import jax
import jax.numpy as jnp
from jax import lax
from jax.experimental import pallas as pl
from jax.experimental.pallas import tpu as pltpu
from jax.sharding import Mesh, PartitionSpec as P

N = 8192
SWEEPS = 10
NEVER = -3.0e38

GROUP = ("xh", "core")
PLANE = ("xl", "y")
LAYER = ("xh", "core", "xl", "y")


def sent_to_all(value, axes):
    length = lax.axis_size(axes)
    return lax.all_to_all(
        jnp.broadcast_to(value[None], (length, *value.shape)), axes, 0, 0, tiled=True
    )


def in_spin_order(gathered):
    n_core, n_xl, n_y, n_z, piece, width = gathered.shape
    shape = (n_z, n_core * n_y, piece, n_xl * width)

    def body(source, target, sems):
        copies = [
            pltpu.make_async_copy(
                source.at[core, xl, y],
                target.at[:, core * n_y + y, :, pl.ds(xl * width, width)],
                sems.at[core, xl, y],
            )
            for xl in range(n_xl)
            for core in range(n_core)
            for y in range(n_y)
        ]
        for copy in copies:
            copy.start()
        for copy in copies:
            copy.wait()

    ordered = pl.pallas_call(
        body,
        in_specs=[pl.BlockSpec(memory_space=pltpu.HBM)],
        out_specs=pl.BlockSpec(memory_space=pl.ANY),
        out_shape=jax.ShapeDtypeStruct(shape, gathered.dtype),
        scratch_shapes=[pltpu.SemaphoreType.DMA((n_core, n_xl, n_y))],
        compiler_params=pltpu.CompilerParams(vmem_limit_bytes=2 * 1024 * 1024),
        name="in_spin_order",
    )(pltpu.with_memory_space_constraint(gathered, pltpu.HBM))
    return ordered.reshape(-1, n_xl * width)


def left_lanes(shape):
    return lax.broadcasted_iota(jnp.int32, shape, len(shape) - 1) < shape[-1] // 2


def packed(value):
    half = value.shape[0] // 2
    return jnp.concatenate([value[:half], value[half:]], axis=1)


def first_terms(spins, blocks, core, xl, count):
    n_core, rows, width = blocks.shape
    half = spins.shape[0] // 2
    lanes = 2 * (n_core * rows // count)
    pairs = count // 2 // n_core

    def body(core_ref, xl_ref, spins_ref, blocks_ref, out_ref, one_ref, two_ref, held_ref, sems):
        arrive = [
            pltpu.make_async_copy(blocks_ref.at[n], held_ref.at[n], sems.at[n])
            for n in range(n_core)
        ]
        for copy in arrive:
            copy.start()
        for copy in arrive:
            copy.wait()
        leave = [
            pltpu.make_async_copy(held_ref.at[core_ref[0]], one_ref, sems.at[n_core]),
            pltpu.make_async_copy(held_ref.at[1 - xl_ref[0]], two_ref, sems.at[n_core + 1]),
        ]
        for copy in leave:
            copy.start()
        is_left = left_lanes((half, lanes))
        for n in range(n_core):
            terms = lax.dot_general(
                spins_ref[...],
                held_ref[n],
                (((1,), (1,)), ((), ())),
                preferred_element_type=jnp.float32,
            )
            for pair in range(pairs):
                both = terms[:, pair * lanes : (pair + 1) * lanes]
                top, bottom = both[:half], both[half:]
                even = jnp.where(is_left, top, pltpu.roll(bottom, lanes // 2, 1))
                odd = jnp.where(is_left, pltpu.roll(top, lanes // 2, 1), bottom)
                at = 2 * (n * pairs + pair)
                out_ref[at] = even.astype(jnp.bfloat16)
                out_ref[at + 1] = odd.astype(jnp.bfloat16)
        for copy in leave:
            copy.wait()

    return pl.pallas_call(
        body,
        in_specs=[
            pl.BlockSpec(memory_space=pltpu.SMEM),
            pl.BlockSpec(memory_space=pltpu.SMEM),
            pl.BlockSpec(memory_space=pltpu.VMEM),
            pl.BlockSpec(memory_space=pl.ANY),
        ],
        out_specs=[pl.BlockSpec(memory_space=pltpu.VMEM)]
        + [pl.BlockSpec(memory_space=pl.ANY)] * 2,
        out_shape=[jax.ShapeDtypeStruct((count, half, lanes), jnp.bfloat16)]
        + [jax.ShapeDtypeStruct((rows, width), jnp.bfloat16)] * 2,
        scratch_shapes=[
            pltpu.VMEM((n_core, rows, width), jnp.bfloat16),
            pltpu.SemaphoreType.DMA((n_core + 2,)),
        ],
        compiler_params=pltpu.CompilerParams(vmem_limit_bytes=16 * 1024 * 1024),
        name="first_terms",
    )(core[None], xl[None], spins, pltpu.with_memory_space_constraint(blocks, pltpu.HBM))


def second_terms(rows, own_spins, blocks, own, far, parts):
    count, half, lanes = rows.shape
    depth, width = far.shape
    share = 2 * half // parts

    def body(own_ref, rows_ref, piece_ref, blocks_ref, far_ref, out_ref, all_ref, held_ref, sems):
        arrive = [
            pltpu.make_async_copy(blocks_ref.at[own_ref[0]], held_ref.at[0], sems.at[0]),
            pltpu.make_async_copy(far_ref, held_ref.at[1], sems.at[1]),
        ]
        for copy in arrive:
            copy.start()
        is_left = left_lanes((half, lanes))
        for pair in range(count // 2):
            even = rows_ref[2 * pair].astype(jnp.float32)
            odd = rows_ref[2 * pair + 1].astype(jnp.float32)
            top = jnp.where(is_left, even, pltpu.roll(odd, lanes // 2, 1))
            bottom = jnp.where(is_left, pltpu.roll(even, lanes // 2, 1), odd)
            at = pl.ds(pair * lanes, lanes)
            all_ref[0:half, at] = top.astype(jnp.bfloat16)
            all_ref[half : 2 * half, at] = bottom.astype(jnp.bfloat16)
        piece = piece_ref[...]
        beside = pl.ds(2 * width, lanes)
        out_ref[0 : parts // 2, :, beside] = piece.reshape(parts // 2, share, lanes)
        piece = pltpu.roll(piece, lanes // 2, 1)
        out_ref[parts // 2 : parts, :, beside] = piece.reshape(parts // 2, share, lanes)
        for n, copy in enumerate(arrive):
            copy.wait()
            terms = jnp.dot(all_ref[...], held_ref[n], preferred_element_type=jnp.float32)
            out_ref[:, :, n * width : (n + 1) * width] = terms.reshape(parts, share, width)

    return pl.pallas_call(
        body,
        out_shape=jax.ShapeDtypeStruct((parts, share, 2 * width + lanes), jnp.float32),
        in_specs=[
            pl.BlockSpec(memory_space=pltpu.SMEM),
            pl.BlockSpec(memory_space=pltpu.VMEM),
            pl.BlockSpec(memory_space=pltpu.VMEM),
            pl.BlockSpec(memory_space=pl.ANY),
            pl.BlockSpec(memory_space=pl.ANY),
        ],
        scratch_shapes=[
            pltpu.VMEM((2 * half, depth), jnp.bfloat16),
            pltpu.VMEM((2, depth, width), jnp.bfloat16),
            pltpu.SemaphoreType.DMA((2,)),
        ],
        compiler_params=pltpu.CompilerParams(vmem_limit_bytes=16 * 1024 * 1024),
        name="second_terms",
    )(own[None], rows, own_spins, pltpu.with_memory_space_constraint(blocks, pltpu.HBM), far)


def per_device(spin_init, couplings, flip_noise, colors, beta_steps, partners, swap_noise):
    rep_dev, row_width = spin_init.shape
    n_xl = lax.axis_size("xl")
    n_y = lax.axis_size("y")
    n_z = lax.axis_size("z")
    n_core = lax.axis_size("core")
    y_index = lax.axis_index("y")
    xl_index = lax.axis_index("xl")
    core_index = lax.axis_index("core")
    rep_index = lax.axis_index(GROUP)
    share = rep_dev // (n_xl * n_y)
    piece = row_width // n_y
    width = n_xl * row_width
    own_block = couplings.reshape(-1, row_width)

    first_slot = rep_index * rep_dev

    def metropolis(spins, fields, limit, scale):
        energy_cost = scale * (spins * fields)
        return jnp.where(energy_cost < limit, -spins, spins)

    blocks = own_block.reshape(n_core, -1, row_width)
    terms, core_half, cross = first_terms(
        spin_init, blocks, core_index, xl_index, n_xl * n_z
    )
    gathered = lax.all_gather(core_half, ("core", *PLANE))
    terms = lax.all_to_all(terms, ("xl", "z"), 0, 0, tiled=True)
    far = lax.ppermute(cross, ("xh", "xl"), [(0, 3), (3, 0), (1, 2), (2, 1)])
    all_betas = beta_steps.astype(jnp.float32)
    all_scales = all_betas * (1.0 / 16384.0)

    def scales(first, length):
        return lax.dynamic_slice_in_dim(all_scales, first, length)[:, None]

    slot_ids = first_slot + jnp.arange(rep_dev, dtype=jnp.int32)
    mate_ids = lax.dynamic_slice_in_dim(partners, first_slot, rep_dev)
    all_ids = jnp.arange(partners.shape[0], dtype=jnp.int32)[None, :]

    def picked(values, ids):
        return jnp.sum(jnp.where(ids[:, None] == all_ids, values[None, :], 0.0), axis=1)

    beta_gap = picked(all_betas, slot_ids) - picked(all_betas, mate_ids)
    noise = picked(swap_noise, jnp.minimum(slot_ids, mate_ids))
    mate_rows_of = (mate_ids[:, None] == all_ids).astype(jnp.bfloat16)

    def own_piece(value):
        return lax.dynamic_slice_in_dim(value, y_index * piece, piece, value.ndim - 1)

    limit = jnp.where(own_piece(colors)[None, :] == 0, own_piece(flip_noise[0]), NEVER)
    fields = terms.astype(jnp.float32).sum(axis=0)
    own_spins = packed(own_piece(spin_init)).astype(jnp.float32)
    own_scales = packed(jnp.broadcast_to(scales(first_slot, rep_dev), (rep_dev, piece)))
    own_spins = metropolis(own_spins, fields, packed(limit), own_scales)


    steps = jnp.arange(1, SWEEPS, dtype=jnp.int32)[:, None, None]

    def limits_of(xl):
        first = (xl * n_y + y_index) * share
        noise = lax.dynamic_slice_in_dim(flip_noise, first, share, 1)[1:]
        return jnp.where(colors[None, None, :] == steps % 2, noise, NEVER)

    is_left = xl_index == 0
    kept = limits_of(xl_index)
    other = limits_of(1 - xl_index)
    other = lax.ppermute(other, "xl", [(0, 1), (1, 0)])
    limits = jnp.concatenate(
        [jnp.where(is_left, kept, other), jnp.where(is_left, other, kept)], axis=2
    )
    limits = [limits[step] for step in range(SWEEPS - 1)]
    scale = scales(first_slot + lax.axis_index(PLANE) * share, share)

    own_spins, limits, scale, beta_gap, noise, mate_rows_of = lax.optimization_barrier(
        (own_spins, limits, scale, beta_gap, noise, mate_rows_of)
    )
    rows = sent_to_all(own_spins.astype(jnp.bfloat16), "z")
    partial = second_terms(rows, own_spins, blocks, xl_index, far, n_xl * n_y)
    partial = lax.all_to_all(partial, PLANE, 0, 0, tiled=True)
    fields = partial.reshape(n_xl, n_y, share, -1).sum(axis=1)
    fields = jnp.concatenate(
        [
            fields[side, :, :row_width] + fields[1 - side, :, row_width:width]
            for side in range(n_xl)
        ],
        axis=1,
    )
    spins = partial[:, :, width : width + piece]
    spins = spins.transpose(1, 0, 2).reshape(share, width)

    def layer_rows(spins):
        return sent_to_all(spins.astype(jnp.bfloat16), "z")

    def layer_fields(rows, layer_block):
        rows = rows.transpose(1, 0, 2).reshape(share, N)
        return jnp.dot(rows, layer_block, preferred_element_type=jnp.float32)

    spins = metropolis(spins, fields, limits[0], scale)
    spins = lax.optimization_barrier(spins)
    rows, gathered = lax.optimization_barrier((layer_rows(spins), gathered))
    layer_block = in_spin_order(
        gathered.reshape(n_core, n_xl, n_y, n_z, piece, row_width)
    )
    for limit in limits[1:]:
        spins = metropolis(spins, layer_fields(rows, layer_block), limit, scale)
        spins = lax.optimization_barrier(spins)
        rows = layer_rows(spins)

    layer_sum = jnp.sum(spins * layer_fields(rows, layer_block), axis=1, keepdims=True)
    layer_sum = jnp.broadcast_to(layer_sum, (share, 128))
    energy = -0.5 * sent_to_all(layer_sum, "z").sum(axis=0)

    high = lax.reduce_precision(energy, 8, 7)
    middle = lax.reduce_precision(energy - high, 8, 7)
    low = (energy - high) - middle
    terms = jnp.concatenate([high[:, :1], middle[:, :1], low[:, :126]], axis=1)
    blocks = spins.astype(jnp.bfloat16).reshape(share, n_xl, row_width).transpose(1, 0, 2)
    terms = jnp.broadcast_to(terms.astype(jnp.bfloat16)[None], (n_xl, share, 128))
    blocks = jnp.concatenate([blocks, terms], axis=2)
    blocks = jnp.broadcast_to(
        blocks[None, :, None], (lax.axis_size(GROUP), n_xl, n_y, *blocks.shape[1:])
    ).reshape(-1, *blocks.shape[1:])
    table = lax.all_to_all(blocks, LAYER, 0, 0, tiled=True).reshape(-1, row_width + 128)

    own_rows = lax.dynamic_slice_in_dim(table, first_slot, rep_dev, 0)
    own_rows = own_rows.astype(jnp.float32)
    mate_rows = jnp.dot(mate_rows_of, table, preferred_element_type=jnp.float32)

    def energy_of(rows):
        return rows[:, row_width] + (rows[:, row_width + 1] + rows[:, row_width + 2])

    own_energy = energy_of(own_rows)
    mate_energy = energy_of(mate_rows)
    swap_gain = beta_gap * (own_energy - mate_energy) * (1.0 / (64.0 * N * math.sqrt(N)))
    accept = swap_gain + noise > 0.0
    spins_out = jnp.where(
        accept[:, None], mate_rows[:, :row_width], own_rows[:, :row_width]
    )
    energies = jnp.where(accept, mate_energy, own_energy) * (1.0 / (N * math.sqrt(N)))
    return (spins_out.astype(jnp.bfloat16), energies)


def solution(mesh):
    fine = Mesh(mesh.devices.reshape(2, 2, 2, 16, 4), ("xh", "core", "xl", "z", "y"))
    rep, row, col = ("xh", "core"), ("xl", "z"), "y"
    in_specs = (
        P(rep, row),
        P(None, col, None, row),
        P(None, rep, row),
        P(row),
        P(),
        P(),
        P(),
    )
    out_specs = (P(rep, row), P(rep))
    return jax.shard_map(
        per_device, mesh=fine, in_specs=in_specs, out_specs=out_specs, check_vma=False
    )
```

profile of v0, /device:TPU:1, one launch (start us, length us, event | category | flops | bytes accessed | tf_op | source)
XLA Modules:
  0.0 292.6 jit_solution(14718730290822477914)
XLA Ops:
  7.2 0.7 copy-done
  8.0 2.8 first_terms.1
  10.8 0.8 broadcast_compare_fusion
  11.6 0.9 dynamic-slice_select_fusion
  12.5 3.9 %collective-permute-start = (f32[9,8,256]{2,1,0:T(8,128)S(1)}, f32[9,8,256]{2,1,0:T(8,128)S(1)}, u32[]{:S(2)}, u32[]{:S(2)}) collective-permute-start(f32[9,8,256]{2,1,0:T(8,128)S(1)} %dynamic-slice_select_fusion), channel_id=1, source_target_pairs={{0,64},{64,0},{1,65},{65,1},{2,66},{66,2},{3,67},{67,3},{4,68},{68... | collective-permute-start | bytes 221192 | tf_op jit(solution)/shard_map/ppermute | solution.py:244
  16.4 15.2 %all-to-all-start = ((bf16[32,32,128]{2,1,0:T(8,128)(2,1)}), bf16[32,32,128]{2,1,0:T(8,128)(2,1)S(1)}, u32[]{:S(2)}, u32[]{:S(2)}) async-start(bf16[32,32,128]{2,1,0:T(8,128)(2,1)} %get-tuple-element.21), calls=%async_computation | async-start | bytes 524288 | tf_op jit(solution)/shard_map/all_to_all | solution.py:205
  31.7 4.7 %collective-permute-start.1 = (bf16[1024,256]{1,0:T(8,128)(2,1)S(1)}, bf16[1024,256]{1,0:T(8,128)(2,1)S(1)}, u32[]{:S(2)}, u32[]{:S(2)}) collective-permute-start(bf16[1024,256]{1,0:T(8,128)(2,1)S(1)} %get-tuple-element.25), channel_id=1, source_target_pairs={{0,320},{320,0},{64,256},{256,64},{1,321},{321,1},{65,257},{257,65... | collective-permute-start | bytes 1572872 | tf_op jit(solution)/shard_map/ppermute | solution.py:206
  36.4 0.8 slice.112
  37.2 0.7 convert_element_type.54
  37.9 0.7 broadcast_multiply_fusion
  38.6 0.1 dynamic_slice.29
  38.7 0.8 fusion.60
  39.4 0.2 select_reduce_fusion.1
  39.6 0.8 constant_dynamic-slice_fusion
  40.4 0.9 select_reduce_fusion
  41.3 0.1 fusion.62
  41.3 0.1 fusion.26
  41.4 0.8 dynamic-slice_compare_fusion
  42.2 0.1 bitcast_select_fusion
  42.3 0.1 dynamic-slice_bitcast_fusion
  42.4 0.9 fusion.27
  43.3 8.1 %all-to-all-done = bf16[32,32,128]{2,1,0:T(8,128)(2,1)S(1)} async-done(((bf16[32,32,128]{2,1,0:T(8,128)(2,1)}), bf16[32,32,128]{2,1,0:T(8,128)(2,1)S(1)}, u32[]{:S(2)}, u32[]{:S(2)}) %all-to-all-start) | async-done | bytes 262176 | tf_op jit(solution)/shard_map/all_to_all | solution.py:205
  51.5 0.1 broadcast_in_dim.89
  51.5 0.1 broadcast_in_dim.90
  51.6 0.1 negate_select_fusion.1.piece_ref
  51.7 0.7 broadcast_in_dim.174
  52.4 4.9 %all-to-all-start.1 = ((bf16[16,32,128]{2,1,0:T(8,128)(2,1)}), bf16[16,32,128]{2,1,0:T(8,128)(2,1)S(1)}, u32[]{:S(2)}, u32[]{:S(2)}) async-start(bf16[16,32,128]{2,1,0:T(8,128)(2,1)} %broadcast_in_dim.174), calls=%async_computation.1 | async-start | bytes 262144 | tf_op jit(solution)/shard_map/all_to_all | solution.py:21
  57.3 12.0 %all-to-all-done.1.rows_ref = bf16[16,32,128]{2,1,0:T(8,128)(2,1)S(1)} async-done(((bf16[16,32,128]{2,1,0:T(8,128)(2,1)}), bf16[16,32,128]{2,1,0:T(8,128)(2,1)S(1)}, u32[]{:S(2)}, u32[]{:S(2)}) %all-to-all-start.1) | async-done | bytes 131104 | tf_op jit(solution)/shard_map/all_to_all | solution.py:21
  69.3 1.6 second_terms.1
  70.9 9.6 %all_to_all.70 = f32[8,8,640]{2,1,0:T(8,128)S(1)} all-to-all(f32[8,8,640]{2,1,0:T(8,128)S(1)} %second_terms.1), channel_id=1, replica_groups=mesh['xh'=2,'core'=2,'xl'=2,'z'=16,'y'=4] {'xl','y'}, dimensions={0} | all-to-all | bytes 327680 | tf_op jit(solution)/shard_map/all_to_all | solution.py:256
  80.5 0.1 reshape.155
  80.6 0.1 negate_select_fusion
  80.7 18.3 %all_to_all.71 = bf16[16,8,512]{2,1,0:T(8,128)(2,1)S(1)} all-to-all(bf16[16,8,512]{2,1,0:T(8,128)(2,1)S(1)} %broadcast_in_dim.175), channel_id=1, replica_groups=mesh['xh'=2,'core'=2,'xl'=2,'z'=16,'y'=4] {'z'}, dimensions={0} | all-to-all | bytes 262144 | tf_op jit(solution)/shard_map/all_to_all | solution.py:21
  99.0 3.5 %in_spin_order.1 = bf16[16,8,64,512]{3,2,1,0:T(8,128)(2,1)S(1)} custom-call(bf16[2,2,4,16,64,256]{5,4,3,2,1,0:T(8,128)(2,1)} %bitcast.102), custom_call_target="tpu_custom_call" | custom-call | tf_op jit(solution)/shard_map/in_spin_order/pallas_call | solution.py:46
  102.5 1.2 fusion.9
  103.7 15.9 %all_to_all.72 = bf16[16,8,512]{2,1,0:T(8,128)(2,1)S(1)} all-to-all(bf16[16,8,512]{2,1,0:T(8,128)(2,1)S(1)} %broadcast_in_dim.176), channel_id=1, replica_groups=mesh['xh'=2,'core'=2,'xl'=2,'z'=16,'y'=4] {'z'}, dimensions={0} | all-to-all | bytes 262144 | tf_op jit(solution)/shard_map/all_to_all | solution.py:21
  119.6 1.1 fusion.11
  120.8 0.1 broadcast_in_dim.177
  120.8 15.8 %all_to_all.73 = bf16[16,8,512]{2,1,0:T(8,128)(2,1)S(1)} all-to-all(bf16[16,8,512]{2,1,0:T(8,128)(2,1)S(1)} %broadcast_in_dim.177), channel_id=1, replica_groups=mesh['xh'=2,'core'=2,'xl'=2,'z'=16,'y'=4] {'z'}, dimensions={0} | all-to-all | bytes 262144 | tf_op jit(solution)/shard_map/all_to_all | solution.py:21
  136.6 1.1 fusion.13
  137.7 0.1 broadcast_in_dim.178
  137.8 15.8 %all_to_all.74 = bf16[16,8,512]{2,1,0:T(8,128)(2,1)S(1)} all-to-all(bf16[16,8,512]{2,1,0:T(8,128)(2,1)S(1)} %broadcast_in_dim.178), channel_id=1, replica_groups=mesh['xh'=2,'core'=2,'xl'=2,'z'=16,'y'=4] {'z'}, dimensions={0} | all-to-all | bytes 262144 | tf_op jit(solution)/shard_map/all_to_all | solution.py:21
  153.6 1.1 fusion.15
  154.8 15.8 %all_to_all.75 = bf16[16,8,512]{2,1,0:T(8,128)(2,1)S(1)} all-to-all(bf16[16,8,512]{2,1,0:T(8,128)(2,1)S(1)} %broadcast_in_dim.179), channel_id=1, replica_groups=mesh['xh'=2,'core'=2,'xl'=2,'z'=16,'y'=4] {'z'}, dimensions={0} | all-to-all | bytes 262144 | tf_op jit(solution)/shard_map/all_to_all | solution.py:21
  170.6 1.1 fusion.17
  171.8 0.1 broadcast_in_dim.180
  171.8 15.6 %all_to_all.76 = bf16[16,8,512]{2,1,0:T(8,128)(2,1)S(1)} all-to-all(bf16[16,8,512]{2,1,0:T(8,128)(2,1)S(1)} %broadcast_in_dim.180), channel_id=1, replica_groups=mesh['xh'=2,'core'=2,'xl'=2,'z'=16,'y'=4] {'z'}, dimensions={0} | all-to-all | bytes 262144 | tf_op jit(solution)/shard_map/all_to_all | solution.py:21
  187.4 1.1 fusion.19
  188.6 15.4 %all_to_all.77 = bf16[16,8,512]{2,1,0:T(8,128)(2,1)S(1)} all-to-all(bf16[16,8,512]{2,1,0:T(8,128)(2,1)S(1)} %broadcast_in_dim.181), channel_id=1, replica_groups=mesh['xh'=2,'core'=2,'xl'=2,'z'=16,'y'=4] {'z'}, dimensions={0} | all-to-all | bytes 262144 | tf_op jit(solution)/shard_map/all_to_all | solution.py:21
  204.1 1.1 fusion.21
  205.2 0.1 broadcast_in_dim.182
  205.3 15.6 %all_to_all.78 = bf16[16,8,512]{2,1,0:T(8,128)(2,1)S(1)} all-to-all(bf16[16,8,512]{2,1,0:T(8,128)(2,1)S(1)} %broadcast_in_dim.182), channel_id=1, replica_groups=mesh['xh'=2,'core'=2,'xl'=2,'z'=16,'y'=4] {'z'}, dimensions={0} | all-to-all | bytes 262144 | tf_op jit(solution)/shard_map/all_to_all | solution.py:21
  220.9 1.1 fusion.23
  222.2 15.5 %all_to_all.79 = bf16[16,8,512]{2,1,0:T(8,128)(2,1)S(1)} all-to-all(bf16[16,8,512]{2,1,0:T(8,128)(2,1)S(1)} %broadcast_in_dim.183), channel_id=1, replica_groups=mesh['xh'=2,'core'=2,'xl'=2,'z'=16,'y'=4] {'z'}, dimensions={0} | all-to-all | bytes 262144 | tf_op jit(solution)/shard_map/all_to_all | solution.py:21
  237.7 1.3 fusion.24
  239.0 0.1 broadcast_in_dim_broadcast_in_dim_broadcast_in_dim.2
  239.0 15.6 %all_to_all.80 = f32[16,8,128]{2,1,0:T(8,128)S(1)} all-to-all(f32[16,8,128]{2,1,0:T(8,128)S(1)} %broadcast_in_dim_broadcast_in_dim_broadcast_in_dim.2), channel_id=1, replica_groups=mesh['xh'=2,'core'=2,'xl'=2,'z'=16,'y'=4] {'z'}, dimensions={0} | all-to-all | bytes 131072 | tf_op jit(solution)/shard_map/all_to_all | solution.py:21
  254.7 0.1 pad_maximum_fusion.2
  254.8 29.2 %all_to_all.81 = bf16[32,8,384]{2,1,0:T(8,128)(2,1)S(1)} all-to-all(bf16[32,8,384]{2,1,0:T(8,128)(2,1)S(1)} %bitcast.114), channel_id=1, replica_groups=mesh['xh'=2,'core'=2,'xl'=2,'z'=16,'y'=4] {'xh','core','xl','y'}, dimensions={0} | all-to-all | bytes 393216 | tf_op jit(solution)/shard_map/all_to_all | solution.py:300
  284.0 0.2 fusion.58
  284.1 0.2 fusion.30
  284.3 0.2 fusion.32
  284.5 0.5 select_multiply_fusion
  285.1 0.7 fusion.25
  (36 shorter events, 0.5 us)
Async XLA Ops:
  7.2 91.8 %all-gather.3.cloned.1.call-start = ((), (), s32[]{:S(2)}) async-start(), calls=%async_computation.14 | async-start | bytes 8912896 | tf_op jit(solution)/shard_map/all_gather | solution.py:204
  7.2 0.8 copy-start
  12.5 29.9 %collective-permute-start = (f32[9,8,256]{2,1,0:T(8,128)S(1)}, f32[9,8,256]{2,1,0:T(8,128)S(1)}, u32[]{:S(2)}, u32[]{:S(2)}) collective-permute-start(f32[9,8,256]{2,1,0:T(8,128)S(1)} %dynamic-slice_select_fusion), channel_id=1, source_target_pairs={{0,64},{64,0},{1,65},{65,1},{2,66},{66,2},{3,67},{67,3},{4,68},{68... | collective-permute-start | bytes 221192 | tf_op jit(solution)/shard_map/ppermute | solution.py:244
  16.4 35.0 %all-to-all-start = ((bf16[32,32,128]{2,1,0:T(8,128)(2,1)}), bf16[32,32,128]{2,1,0:T(8,128)(2,1)S(1)}, u32[]{:S(2)}, u32[]{:S(2)}) async-start(bf16[32,32,128]{2,1,0:T(8,128)(2,1)} %get-tuple-element.21), calls=%async_computation | async-start | bytes 524288 | tf_op jit(solution)/shard_map/all_to_all | solution.py:205
  31.7 25.7 %collective-permute-start.1 = (bf16[1024,256]{1,0:T(8,128)(2,1)S(1)}, bf16[1024,256]{1,0:T(8,128)(2,1)S(1)}, u32[]{:S(2)}, u32[]{:S(2)}) collective-permute-start(bf16[1024,256]{1,0:T(8,128)(2,1)S(1)} %get-tuple-element.25), channel_id=1, source_target_pairs={{0,320},{320,0},{64,256},{256,64},{1,321},{321,1},{65,257},{257,65... | collective-permute-start | bytes 1572872 | tf_op jit(solution)/shard_map/ppermute | solution.py:206
  52.4 16.9 %all-to-all-start.1 = ((bf16[16,32,128]{2,1,0:T(8,128)(2,1)}), bf16[16,32,128]{2,1,0:T(8,128)(2,1)S(1)}, u32[]{:S(2)}, u32[]{:S(2)}) async-start(bf16[16,32,128]{2,1,0:T(8,128)(2,1)} %broadcast_in_dim.174), calls=%async_computation.1 | async-start | bytes 262144 | tf_op jit(solution)/shard_map/all_to_all | solution.py:21
Sparse Core Ops, SparseCore 0:
  10.9 68.0 all-gather.2
where the time goes:
time: 294 us; the launch traced here: 293 us
  blocking collectives  198 us (67%)
  starting transfers between devices  28.8 us (10%)
  waiting for transfers between devices  20.1 us (7%)
  between operations  14.3 us (5%)
  matrix products  10.7 us (4%)
  other arithmetic  8.67 us (3%)
  Pallas kernels  7.93 us (3%)
  local copies, waits for them, and re-layouts  4.06 us (1%)
    all_to_all x10, blocking collectives, sent_to_all(): lax.all_to_all(jnp.broadcast_to(value[None], (length, *value.shape)), axe...  159 us
    all_to_all x1, blocking collectives, per_device(): lax.all_to_all(blocks, LAYER, 0, 0, tiled=True).reshape(-1, row_width + 128)  29.2 us
    all_to_all x1, starting transfers between devices, per_device(): terms = lax.all_to_all(terms, ('xl', 'z'), 0, 0, tiled=True)  15.2 us
    all_to_all x1, waiting for transfers between devices, sent_to_all(): lax.all_to_all(jnp.broadcast_to(value[None], (length, *value.shape)), axe...  12 us
    dot_general x9, matrix products, layer_fields(): return jnp.dot(rows, layer_block, preferred_element_type=jnp.float32)  10.5 us
    all_to_all x1, blocking collectives, per_device(): partial = lax.all_to_all(partial, PLANE, 0, 0, tiled=True)  9.58 us
    all_to_all x1, waiting for transfers between devices, per_device(): terms = lax.all_to_all(terms, ('xl', 'z'), 0, 0, tiled=True)  8.13 us
  transfers between devices with their start and end apart: 5, of which 2 were waited for; matrix products, arithmetic and copies ran while one was open for 3% of the time, Pallas kernels for 1%

commit v1 on v0

--- a/solution.py
+++ b/solution.py
@@ -70,25 +70,30 @@
     lanes = 2 * (n_core * rows // count)
     pairs = count // 2 // n_core
 
-    def body(core_ref, xl_ref, spins_ref, blocks_ref, out_ref, one_ref, two_ref, held_ref, sems):
+    def body(
+        core_ref, xl_ref, spins_ref, blocks_ref, out_ref, one_ref, two_ref, spins_held, held_ref, sems
+    ):
+        spins_arrive = pltpu.make_async_copy(spins_ref, spins_held, sems.at[n_core + 2])
         arrive = [
             pltpu.make_async_copy(blocks_ref.at[n], held_ref.at[n], sems.at[n])
             for n in range(n_core)
         ]
+        spins_arrive.start()
         for copy in arrive:
             copy.start()
-        for copy in arrive:
-            copy.wait()
         leave = [
             pltpu.make_async_copy(held_ref.at[core_ref[0]], one_ref, sems.at[n_core]),
             pltpu.make_async_copy(held_ref.at[1 - xl_ref[0]], two_ref, sems.at[n_core + 1]),
         ]
-        for copy in leave:
-            copy.start()
+        spins_arrive.wait()
         is_left = left_lanes((half, lanes))
         for n in range(n_core):
+            arrive[n].wait()
+            if n == n_core - 1:
+                for copy in leave:
+                    copy.start()
             terms = lax.dot_general(
-                spins_ref[...],
+                spins_held[...],
                 held_ref[n],
                 (((1,), (1,)), ((), ())),
                 preferred_element_type=jnp.float32,
@@ -109,7 +114,7 @@
         in_specs=[
             pl.BlockSpec(memory_space=pltpu.SMEM),
             pl.BlockSpec(memory_space=pltpu.SMEM),
-            pl.BlockSpec(memory_space=pltpu.VMEM),
+            pl.BlockSpec(memory_space=pl.ANY),
             pl.BlockSpec(memory_space=pl.ANY),
         ],
         out_specs=[pl.BlockSpec(memory_space=pltpu.VMEM)]
@@ -117,12 +122,18 @@
         out_shape=[jax.ShapeDtypeStruct((count, half, lanes), jnp.bfloat16)]
         + [jax.ShapeDtypeStruct((rows, width), jnp.bfloat16)] * 2,
         scratch_shapes=[
+            pltpu.VMEM(spins.shape, jnp.bfloat16),
             pltpu.VMEM((n_core, rows, width), jnp.bfloat16),
-            pltpu.SemaphoreType.DMA((n_core + 2,)),
+            pltpu.SemaphoreType.DMA((n_core + 3,)),
         ],
         compiler_params=pltpu.CompilerParams(vmem_limit_bytes=16 * 1024 * 1024),
         name="first_terms",
-    )(core[None], xl[None], spins, pltpu.with_memory_space_constraint(blocks, pltpu.HBM))
+    )(
+        core[None],
+        xl[None],
+        pltpu.with_memory_space_constraint(spins, pltpu.HBM),
+        pltpu.with_memory_space_constraint(blocks, pltpu.HBM),
+    )
 
 
 def second_terms(rows, own_spins, blocks, own, far, parts):
@@ -176,6 +187,41 @@
     )(own[None], rows, own_spins, pltpu.with_memory_space_constraint(blocks, pltpu.HBM), far)
 
 
+def last_blocks(energy_rows, spins, group, sides, others):
+    share, width = spins.shape
+    part = width // sides
+    lanes = energy_rows.shape[1]
+    count = group * sides * others
+
+    def body(rows_ref, spins_ref, out_ref):
+        row = -0.5 * jnp.sum(rows_ref[...], axis=0, keepdims=True)
+        lane = lax.broadcasted_iota(jnp.int32, (share, lanes), 1)
+        sublane = lax.broadcasted_iota(jnp.int32, (share, lanes), 0)
+        energy = jnp.sum(
+            jnp.where(lane == sublane, jnp.broadcast_to(row, (share, lanes)), 0.0),
+            axis=1,
+            keepdims=True,
+        )
+        energy = jnp.broadcast_to(energy, (share, lanes))
+        high = energy.astype(jnp.bfloat16).astype(jnp.float32)
+        middle = (energy - high).astype(jnp.bfloat16).astype(jnp.float32)
+        low = (energy - high) - middle
+        terms = jnp.where(lane == 0, high, jnp.where(lane == 1, middle, low))
+        terms = terms.astype(jnp.bfloat16)
+        values = spins_ref[...].astype(jnp.bfloat16)
+        for n in range(count):
+            side = n // others % sides
+            out_ref[n, :, 0:part] = values[:, side * part : (side + 1) * part]
+            out_ref[n, :, part : part + lanes] = terms
+
+    return pl.pallas_call(
+        body,
+        out_shape=jax.ShapeDtypeStruct((count, share, part + lanes), jnp.bfloat16),
+        compiler_params=pltpu.CompilerParams(vmem_limit_bytes=8 * 1024 * 1024),
+        name="last_blocks",
+    )(energy_rows, spins)
+
+
 def per_device(spin_init, couplings, flip_noise, colors, beta_steps, partners, swap_noise):
     rep_dev, row_width = spin_init.shape
     n_xl = lax.axis_size("xl")
@@ -248,8 +294,8 @@
     limits = [limits[step] for step in range(SWEEPS - 1)]
     scale = scales(first_slot + lax.axis_index(PLANE) * share, share)
 
-    own_spins, limits, scale, beta_gap, noise, mate_rows_of = lax.optimization_barrier(
-        (own_spins, limits, scale, beta_gap, noise, mate_rows_of)
+    own_spins, limits, scale, beta_gap, noise, mate_rows_of, far = lax.optimization_barrier(
+        (own_spins, limits, scale, beta_gap, noise, mate_rows_of, far)
     )
     rows = sent_to_all(own_spins.astype(jnp.bfloat16), "z")
     partial = second_terms(rows, own_spins, blocks, xl_index, far, n_xl * n_y)
@@ -283,20 +329,10 @@
         spins = lax.optimization_barrier(spins)
         rows = layer_rows(spins)
 
-    layer_sum = jnp.sum(spins * layer_fields(rows, layer_block), axis=1, keepdims=True)
-    layer_sum = jnp.broadcast_to(layer_sum, (share, 128))
-    energy = -0.5 * sent_to_all(layer_sum, "z").sum(axis=0)
-
-    high = lax.reduce_precision(energy, 8, 7)
-    middle = lax.reduce_precision(energy - high, 8, 7)
-    low = (energy - high) - middle
-    terms = jnp.concatenate([high[:, :1], middle[:, :1], low[:, :126]], axis=1)
-    blocks = spins.astype(jnp.bfloat16).reshape(share, n_xl, row_width).transpose(1, 0, 2)
-    terms = jnp.broadcast_to(terms.astype(jnp.bfloat16)[None], (n_xl, share, 128))
-    blocks = jnp.concatenate([blocks, terms], axis=2)
-    blocks = jnp.broadcast_to(
-        blocks[None, :, None], (lax.axis_size(GROUP), n_xl, n_y, *blocks.shape[1:])
-    ).reshape(-1, *blocks.shape[1:])
+    layer_sum = jnp.sum(spins * layer_fields(rows, layer_block), axis=1)
+    layer_sum = jnp.pad(layer_sum, (0, 128 - share))[None]
+    energy_rows = sent_to_all(layer_sum, "z").reshape(n_z, 128)
+    blocks = last_blocks(energy_rows, spins, lax.axis_size(GROUP), n_xl, n_y)
     table = lax.all_to_all(blocks, LAYER, 0, 0, tiled=True).reshape(-1, row_width + 128)
 
     own_rows = lax.dynamic_slice_in_dim(table, first_slot, rep_dev, 0)

time: 294 us -> 296 us (level)
  blocking collectives: 198 us -> 218 us
  waiting for transfers between devices: 20.1 us -> 8.14 us
  starting transfers between devices: 28.8 us -> 23.9 us
    all_to_all x10 -> x11, blocking collectives: 159 us -> 176 us  [sent_to_all(): lax.all_to_all(jnp.broadcast_to(value[None], (length, *value.shape)), axe...]
    all_to_all x1 -> x0, waiting for transfers between devices: 12 us -> none  [sent_to_all(): lax.all_to_all(jnp.broadcast_to(value[None], (length, *value.shape)), axe...]
    all_to_all x1 -> x0, starting transfers between devices: 4.93 us -> none  [sent_to_all(): lax.all_to_all(jnp.broadcast_to(value[None], (length, *value.shape)), axe...]
    all_to_all x1, blocking collectives: 29.2 us -> 32.9 us  [per_device(): lax.all_to_all(blocks, LAYER, 0, 0, tiled=True).reshape(-1, row_width + 128)]
  transfers between devices with their start and end apart: 5 -> 4, of which waited for: 2 -> 1; matrix products, arithmetic and copies ran while one was open for 3% -> 3% of each run, Pallas kernels for 1% -> 1%
where the time goes in v1:
time: 296 us; the launch traced here: 295 us
  blocking collectives  218 us (74%)
  starting transfers between devices  23.9 us (8%)
  between operations  14.3 us (5%)
  matrix products  10.7 us (4%)
  other arithmetic  8.56 us (3%)
  Pallas kernels  8.26 us (3%)
  waiting for transfers between devices  8.14 us (3%)
    all_to_all x11, blocking collectives, sent_to_all(): lax.all_to_all(jnp.broadcast_to(value[None], (length, *value.shape)), axe...  176 us
    all_to_all x1, blocking collectives, per_device(): lax.all_to_all(blocks, LAYER, 0, 0, tiled=True).reshape(-1, row_width + 128)  32.9 us
    all_to_all x1, starting transfers between devices, per_device(): terms = lax.all_to_all(terms, ('xl', 'z'), 0, 0, tiled=True)  15.2 us
    dot_general x9, matrix products, layer_fields(): return jnp.dot(rows, layer_block, preferred_element_type=jnp.float32)  10.5 us
    all_to_all x1, blocking collectives, per_device(): partial = lax.all_to_all(partial, PLANE, 0, 0, tiled=True)  9.6 us
    all_to_all x1, waiting for transfers between devices, per_device(): terms = lax.all_to_all(terms, ('xl', 'z'), 0, 0, tiled=True)  8.12 us
  transfers between devices with their start and end apart: 4, of which 1 were waited for; matrix products, arithmetic and copies ran while one was open for 3% of the time, Pallas kernels for 1%

profile of v1, /device:TPU:1, one launch (start us, length us, event | category | flops | bytes accessed | tf_op | source)
XLA Modules:
  0.0 294.8 jit_solution(14918610800657528254)
XLA Ops:
  7.2 3.0 %first_terms.1 = (bf16[32,32,128]{2,1,0:T(8,128)(2,1)}, bf16[1024,256]{1,0:T(8,128)(2,1)}, bf16[1024,256]{1,0:T(8,128)(2,1)S(1)}) custom-call(s32[1]{0:T(128)} %bitcast.core_ref, s32[1]{0:T(128)} %bitcast.1.xl_ref.own_ref, bf16[64,256]{1,0:T(8,128)(2,1)} %spins_ref.1, bf16[2,1024,256]{2,1,0:T(8,128)(2,1)} %bitcast.98), custom_call_target="tpu_custom_call" | custom-call | tf_op jit(solution)/shard_map/first_terms/pallas_call | solution.py:112
  10.3 0.8 broadcast_compare_fusion
  11.1 0.9 dynamic-slice_select_fusion
  12.0 3.9 %collective-permute-start = (f32[9,8,256]{2,1,0:T(8,128)S(1)}, f32[9,8,256]{2,1,0:T(8,128)S(1)}, u32[]{:S(2)}, u32[]{:S(2)}) collective-permute-start(f32[9,8,256]{2,1,0:T(8,128)S(1)} %dynamic-slice_select_fusion), channel_id=1, source_target_pairs={{0,64},{64,0},{1,65},{65,1},{2,66},{66,2},{3,67},{67,3},{4,68},{68... | collective-permute-start | bytes 221192 | tf_op jit(solution)/shard_map/ppermute | solution.py:290
  15.9 15.2 %all-to-all-start = ((bf16[32,32,128]{2,1,0:T(8,128)(2,1)}), bf16[32,32,128]{2,1,0:T(8,128)(2,1)S(1)}, u32[]{:S(2)}, u32[]{:S(2)}) async-start(bf16[32,32,128]{2,1,0:T(8,128)(2,1)} %get-tuple-element.22), calls=%async_computation | async-start | bytes 524288 | tf_op jit(solution)/shard_map/all_to_all | solution.py:251
  31.1 4.7 %collective-permute-start.1 = (bf16[1024,256]{1,0:T(8,128)(2,1)S(1)}, bf16[1024,256]{1,0:T(8,128)(2,1)S(1)}, u32[]{:S(2)}, u32[]{:S(2)}) collective-permute-start(bf16[1024,256]{1,0:T(8,128)(2,1)S(1)} %get-tuple-element.23), channel_id=1, source_target_pairs={{0,320},{320,0},{64,256},{256,64},{1,321},{321,1},{65,257},{257,65... | collective-permute-start | bytes 1572872 | tf_op jit(solution)/shard_map/ppermute | solution.py:252
  35.8 0.8 slice.100
  36.7 0.7 convert_element_type.50
  37.4 0.7 broadcast_multiply_fusion
  38.1 0.1 dynamic_slice.29
  38.1 0.8 fusion.43
  38.9 0.2 select_reduce_fusion.1
  39.1 0.8 constant_dynamic-slice_fusion
  39.9 0.9 select_reduce_fusion
  40.7 0.1 fusion.45
  40.8 0.1 fusion.10
  40.9 0.8 dynamic-slice_compare_fusion
  41.7 0.1 bitcast_select_fusion
  41.8 0.1 dynamic-slice_bitcast_fusion
  41.8 0.9 fusion.11
  42.8 8.1 %all-to-all-done = bf16[32,32,128]{2,1,0:T(8,128)(2,1)S(1)} async-done(((bf16[32,32,128]{2,1,0:T(8,128)(2,1)}), bf16[32,32,128]{2,1,0:T(8,128)(2,1)S(1)}, u32[]{:S(2)}, u32[]{:S(2)}) %all-to-all-start) | async-done | bytes 262176 | tf_op jit(solution)/shard_map/all_to_all | solution.py:251
  50.9 0.1 broadcast_in_dim.87
  51.0 0.1 broadcast_in_dim.88
  51.1 0.1 negate_select_fusion.9.piece_ref
  51.2 18.3 %all_to_all.70.rows_ref = bf16[16,32,128]{2,1,0:T(8,128)(2,1)S(1)} all-to-all(bf16[16,32,128]{2,1,0:T(8,128)(2,1)S(1)} %broadcast_in_dim.166), channel_id=1, replica_groups=mesh['xh'=2,'core'=2,'xl'=2,'z'=16,'y'=4] {'z'}, dimensions={0} | all-to-all | bytes 262144 | tf_op jit(solution)/shard_map/all_to_all | solution.py:21
  69.5 1.6 second_terms.1
  71.1 9.6 %all_to_all.71 = f32[8,8,640]{2,1,0:T(8,128)S(1)} all-to-all(f32[8,8,640]{2,1,0:T(8,128)S(1)} %second_terms.1), channel_id=1, replica_groups=mesh['xh'=2,'core'=2,'xl'=2,'z'=16,'y'=4] {'xl','y'}, dimensions={0} | all-to-all | bytes 327680 | tf_op jit(solution)/shard_map/all_to_all | solution.py:302
  80.7 0.1 reshape.132
  80.8 0.1 negate_select_fusion.8
  80.9 17.1 %all_to_all.72 = bf16[16,8,512]{2,1,0:T(8,128)(2,1)S(1)} all-to-all(bf16[16,8,512]{2,1,0:T(8,128)(2,1)S(1)} %broadcast_in_dim.167), channel_id=1, replica_groups=mesh['xh'=2,'core'=2,'xl'=2,'z'=16,'y'=4] {'z'}, dimensions={0} | all-to-all | bytes 262144 | tf_op jit(solution)/shard_map/all_to_all | solution.py:21
  98.1 3.5 %in_spin_order.1 = bf16[16,8,64,512]{3,2,1,0:T(8,128)(2,1)S(1)} custom-call(bf16[2,2,4,16,64,256]{5,4,3,2,1,0:T(8,128)(2,1)} %bitcast.97), custom_call_target="tpu_custom_call" | custom-call | tf_op jit(solution)/shard_map/in_spin_order/pallas_call | solution.py:46
  101.6 1.2 negate_select_fusion.7
  102.7 0.1 broadcast_in_dim.168
  102.8 15.9 %all_to_all.73 = bf16[16,8,512]{2,1,0:T(8,128)(2,1)S(1)} all-to-all(bf16[16,8,512]{2,1,0:T(8,128)(2,1)S(1)} %broadcast_in_dim.168), channel_id=1, replica_groups=mesh['xh'=2,'core'=2,'xl'=2,'z'=16,'y'=4] {'z'}, dimensions={0} | all-to-all | bytes 262144 | tf_op jit(solution)/shard_map/all_to_all | solution.py:21
  118.7 1.1 negate_select_fusion.6
  119.8 0.1 broadcast_in_dim.169
  119.9 15.8 %all_to_all.74 = bf16[16,8,512]{2,1,0:T(8,128)(2,1)S(1)} all-to-all(bf16[16,8,512]{2,1,0:T(8,128)(2,1)S(1)} %broadcast_in_dim.169), channel_id=1, replica_groups=mesh['xh'=2,'core'=2,'xl'=2,'z'=16,'y'=4] {'z'}, dimensions={0} | all-to-all | bytes 262144 | tf_op jit(solution)/shard_map/all_to_all | solution.py:21
  135.7 1.1 negate_select_fusion.5
  136.9 0.1 broadcast_in_dim.170
  136.9 15.7 %all_to_all.75 = bf16[16,8,512]{2,1,0:T(8,128)(2,1)S(1)} all-to-all(bf16[16,8,512]{2,1,0:T(8,128)(2,1)S(1)} %broadcast_in_dim.170), channel_id=1, replica_groups=mesh['xh'=2,'core'=2,'xl'=2,'z'=16,'y'=4] {'z'}, dimensions={0} | all-to-all | bytes 262144 | tf_op jit(solution)/shard_map/all_to_all | solution.py:21
  152.6 1.1 negate_select_fusion.4
  153.8 0.1 broadcast_in_dim.171
  153.9 15.6 %all_to_all.76 = bf16[16,8,512]{2,1,0:T(8,128)(2,1)S(1)} all-to-all(bf16[16,8,512]{2,1,0:T(8,128)(2,1)S(1)} %broadcast_in_dim.171), channel_id=1, replica_groups=mesh['xh'=2,'core'=2,'xl'=2,'z'=16,'y'=4] {'z'}, dimensions={0} | all-to-all | bytes 262144 | tf_op jit(solution)/shard_map/all_to_all | solution.py:21
  169.5 1.1 negate_select_fusion.3
  170.6 0.1 broadcast_in_dim.172
  170.7 15.4 %all_to_all.77 = bf16[16,8,512]{2,1,0:T(8,128)(2,1)S(1)} all-to-all(bf16[16,8,512]{2,1,0:T(8,128)(2,1)S(1)} %broadcast_in_dim.172), channel_id=1, replica_groups=mesh['xh'=2,'core'=2,'xl'=2,'z'=16,'y'=4] {'z'}, dimensions={0} | all-to-all | bytes 262144 | tf_op jit(solution)/shard_map/all_to_all | solution.py:21
  186.1 1.1 negate_select_fusion.2
  187.3 0.1 broadcast_in_dim.173
  187.3 15.6 %all_to_all.78 = bf16[16,8,512]{2,1,0:T(8,128)(2,1)S(1)} all-to-all(bf16[16,8,512]{2,1,0:T(8,128)(2,1)S(1)} %broadcast_in_dim.173), channel_id=1, replica_groups=mesh['xh'=2,'core'=2,'xl'=2,'z'=16,'y'=4] {'z'}, dimensions={0} | all-to-all | bytes 262144 | tf_op jit(solution)/shard_map/all_to_all | solution.py:21
  202.9 1.1 negate_select_fusion.1
  204.1 0.1 broadcast_in_dim.174
  204.1 15.7 %all_to_all.79 = bf16[16,8,512]{2,1,0:T(8,128)(2,1)S(1)} all-to-all(bf16[16,8,512]{2,1,0:T(8,128)(2,1)S(1)} %broadcast_in_dim.174), channel_id=1, replica_groups=mesh['xh'=2,'core'=2,'xl'=2,'z'=16,'y'=4] {'z'}, dimensions={0} | all-to-all | bytes 262144 | tf_op jit(solution)/shard_map/all_to_all | solution.py:21
  219.8 1.1 negate_select_fusion.spins_ref
  221.0 0.1 broadcast_in_dim.175
  221.0 16.5 %all_to_all.80 = bf16[16,8,512]{2,1,0:T(8,128)(2,1)S(1)} all-to-all(bf16[16,8,512]{2,1,0:T(8,128)(2,1)S(1)} %broadcast_in_dim.175), channel_id=1, replica_groups=mesh['xh'=2,'core'=2,'xl'=2,'z'=16,'y'=4] {'z'}, dimensions={0} | all-to-all | bytes 262144 | tf_op jit(solution)/shard_map/all_to_all | solution.py:21
  237.6 1.3 fusion.8
  238.9 14.3 %all_to_all.81 = f32[16,1,128]{2,1,0:T(1,128)S(1)} all-to-all(f32[16,1,128]{2,1,0:T(1,128)S(1)} %broadcast_in_dim.176), channel_id=1, replica_groups=mesh['xh'=2,'core'=2,'xl'=2,'z'=16,'y'=4] {'z'}, dimensions={0} | all-to-all | bytes 16384 | tf_op jit(solution)/shard_map/all_to_all | solution.py:21
  253.2 0.1 last_blocks.1
  253.3 32.9 %all_to_all.82 = bf16[32,8,384]{2,1,0:T(8,128)(2,1)S(1)} all-to-all(bf16[32,8,384]{2,1,0:T(8,128)(2,1)S(1)} %last_blocks.1), channel_id=1, replica_groups=mesh['xh'=2,'core'=2,'xl'=2,'z'=16,'y'=4] {'xh','core','xl','y'}, dimensions={0} | all-to-all | bytes 393216 | tf_op jit(solution)/shard_map/all_to_all | solution.py:336
  286.2 0.2 fusion.41
  286.4 0.2 fusion.14
  286.6 0.2 fusion.16
  286.8 0.5 select_multiply_fusion
  287.3 0.7 fusion.9
  (29 shorter events, 0.3 us)
Async XLA Ops:
  7.2 90.9 %all-gather.3.cloned.1.call-start = ((), (), s32[]{:S(2)}) async-start(), calls=%async_computation.14 | async-start | bytes 8912896 | tf_op jit(solution)/shard_map/all_gather | solution.py:250
  12.0 29.9 %collective-permute-start = (f32[9,8,256]{2,1,0:T(8,128)S(1)}, f32[9,8,256]{2,1,0:T(8,128)S(1)}, u32[]{:S(2)}, u32[]{:S(2)}) collective-permute-start(f32[9,8,256]{2,1,0:T(8,128)S(1)} %dynamic-slice_select_fusion), channel_id=1, source_target_pairs={{0,64},{64,0},{1,65},{65,1},{2,66},{66,2},{3,67},{67,3},{4,68},{68... | collective-permute-start | bytes 221192 | tf_op jit(solution)/shard_map/ppermute | solution.py:290
  15.9 35.0 %all-to-all-start = ((bf16[32,32,128]{2,1,0:T(8,128)(2,1)}), bf16[32,32,128]{2,1,0:T(8,128)(2,1)S(1)}, u32[]{:S(2)}, u32[]{:S(2)}) async-start(bf16[32,32,128]{2,1,0:T(8,128)(2,1)} %get-tuple-element.22), calls=%async_computation | async-start | bytes 524288 | tf_op jit(solution)/shard_map/all_to_all | solution.py:251
  31.1 20.0 %collective-permute-start.1 = (bf16[1024,256]{1,0:T(8,128)(2,1)S(1)}, bf16[1024,256]{1,0:T(8,128)(2,1)S(1)}, u32[]{:S(2)}, u32[]{:S(2)}) collective-permute-start(bf16[1024,256]{1,0:T(8,128)(2,1)S(1)} %get-tuple-element.23), channel_id=1, source_target_pairs={{0,320},{320,0},{64,256},{256,64},{1,321},{321,1},{65,257},{257,65... | collective-permute-start | bytes 1572872 | tf_op jit(solution)/shard_map/ppermute | solution.py:252
Sparse Core Ops, SparseCore 0:
  10.4 68.0 all-gather.2

commit v2 on v1

--- a/solution.py
+++ b/solution.py
@@ -294,12 +294,13 @@
     limits = [limits[step] for step in range(SWEEPS - 1)]
     scale = scales(first_slot + lax.axis_index(PLANE) * share, share)
 
-    own_spins, limits, scale, beta_gap, noise, mate_rows_of, far = lax.optimization_barrier(
-        (own_spins, limits, scale, beta_gap, noise, mate_rows_of, far)
-    )
     rows = sent_to_all(own_spins.astype(jnp.bfloat16), "z")
     partial = second_terms(rows, own_spins, blocks, xl_index, far, n_xl * n_y)
-    partial = lax.all_to_all(partial, PLANE, 0, 0, tiled=True)
+    partial, limits, scale, beta_gap, noise, mate_rows_of = lax.optimization_barrier(
+        (partial, limits, scale, beta_gap, noise, mate_rows_of)
+    )
+    partial = lax.all_to_all(partial.astype(jnp.int16), PLANE, 0, 0, tiled=True)
+    partial = partial.astype(jnp.float32)
     fields = partial.reshape(n_xl, n_y, share, -1).sum(axis=1)
     fields = jnp.concatenate(
         [

time: 296 us -> 292 us (0.986)
  blocking collectives: 218 us -> 196 us
  waiting for transfers between devices: 8.14 us -> 20.1 us
  starting transfers between devices: 23.9 us -> 28.8 us
    all_to_all x11 -> x10, blocking collectives: 176 us -> 158 us  [sent_to_all(): lax.all_to_all(jnp.broadcast_to(value[None], (length, *value.shape)), axe...]
    all_to_all x0 -> x1, waiting for transfers between devices: none -> 10.1 us  [sent_to_all(): lax.all_to_all(jnp.broadcast_to(value[None], (length, *value.shape)), axe...]
    all_to_all x0 -> x1, starting transfers between devices: none -> 4.93 us  [sent_to_all(): lax.all_to_all(jnp.broadcast_to(value[None], (length, *value.shape)), axe...]
    all_to_all x1, blocking collectives: 32.9 us -> 29.3 us  [per_device(): lax.all_to_all(blocks, LAYER, 0, 0, tiled=True).reshape(-1, row_width + 128)]
  transfers between devices with their start and end apart: 4 -> 5, of which waited for: 1 -> 2; matrix products, arithmetic and copies ran while one was open for 3% -> 3% of each run, Pallas kernels for 1% -> 1%
where the time goes in v2:
time: 292 us; the launch traced here: 291 us
  blocking collectives  196 us (67%)
  starting transfers between devices  28.8 us (10%)
  waiting for transfers between devices  20.1 us (7%)
  between operations  14.5 us (5%)
  matrix products  10.6 us (4%)
  other arithmetic  8.97 us (3%)
  Pallas kernels  8.27 us (3%)
    all_to_all x10, blocking collectives, sent_to_all(): lax.all_to_all(jnp.broadcast_to(value[None], (length, *value.shape)), axe...  158 us
    all_to_all x1, blocking collectives, per_device(): lax.all_to_all(blocks, LAYER, 0, 0, tiled=True).reshape(-1, row_width + 128)  29.3 us
    all_to_all x1, starting transfers between devices, per_device(): terms = lax.all_to_all(terms, ('xl', 'z'), 0, 0, tiled=True)  15.2 us
    dot_general x9, matrix products, layer_fields(): return jnp.dot(rows, layer_block, preferred_element_type=jnp.float32)  10.5 us
    all_to_all x1, waiting for transfers between devices, sent_to_all(): lax.all_to_all(jnp.broadcast_to(value[None], (length, *value.shape)), axe...  10.1 us
    all_to_all x1, waiting for transfers between devices, per_device(): terms = lax.all_to_all(terms, ('xl', 'z'), 0, 0, tiled=True)  10 us
    all_to_all x1, blocking collectives, per_device(): partial = lax.all_to_all(partial.astype(jnp.int16), PLANE, 0, 0, tiled=True)  9.22 us
  transfers between devices with their start and end apart: 5, of which 2 were waited for; matrix products, arithmetic and copies ran while one was open for 3% of the time, Pallas kernels for 1%

profile of v2, /device:TPU:1, one launch (start us, length us, event | category | flops | bytes accessed | tf_op | source)
XLA Modules:
  0.0 290.6 jit_solution(14089486688454603411)
XLA Ops:
  7.2 0.0 all-gather.3.cloned.1.call-start
  7.2 3.0 %first_terms.1 = (bf16[32,32,128]{2,1,0:T(8,128)(2,1)}, bf16[1024,256]{1,0:T(8,128)(2,1)}, bf16[1024,256]{1,0:T(8,128)(2,1)S(1)}) custom-call(s32[1]{0:T(128)} %bitcast.1.core_ref, s32[1]{0:T(128)} %bitcast.xl_ref.own_ref, bf16[64,256]{1,0:T(8,128)(2,1)} %spins_ref.1, bf16[2,1024,256]{2,1,0:T(8,128)(2,1)} %bitcast.98), custom_call_target="tpu_custom_call" | custom-call | tf_op jit(solution)/shard_map/first_terms/pallas_call | solution.py:112
  10.3 0.0 all-gather.3.cloned.1.call-update
  10.3 0.8 broadcast_compare_fusion
  11.1 0.9 dynamic-slice_select_fusion
  12.0 3.9 %collective-permute-start.1 = (f32[9,8,256]{2,1,0:T(8,128)S(1)}, f32[9,8,256]{2,1,0:T(8,128)S(1)}, u32[]{:S(2)}, u32[]{:S(2)}) collective-permute-start(f32[9,8,256]{2,1,0:T(8,128)S(1)} %dynamic-slice_select_fusion), channel_id=1, source_target_pairs={{0,64},{64,0},{1,65},{65,1},{2,66},{66,2},{3,67},{67,3},{4,68},{68... | collective-permute-start | bytes 221192 | tf_op jit(solution)/shard_map/ppermute | solution.py:290
  15.9 15.2 %all-to-all-start = ((bf16[32,32,128]{2,1,0:T(8,128)(2,1)}), bf16[32,32,128]{2,1,0:T(8,128)(2,1)S(1)}, u32[]{:S(2)}, u32[]{:S(2)}) async-start(bf16[32,32,128]{2,1,0:T(8,128)(2,1)} %get-tuple-element.21), calls=%async_computation | async-start | bytes 524288 | tf_op jit(solution)/shard_map/all_to_all | solution.py:251
  31.1 4.7 %collective-permute-start = (bf16[1024,256]{1,0:T(8,128)(2,1)S(1)}, bf16[1024,256]{1,0:T(8,128)(2,1)S(1)}, u32[]{:S(2)}, u32[]{:S(2)}) collective-permute-start(bf16[1024,256]{1,0:T(8,128)(2,1)S(1)} %get-tuple-element.22), channel_id=1, source_target_pairs={{0,320},{320,0},{64,256},{256,64},{1,321},{321,1},{65,257},{257,65... | collective-permute-start | bytes 1572872 | tf_op jit(solution)/shard_map/ppermute | solution.py:252
  35.8 0.8 fusion.43
  36.6 0.8 constant_dynamic-slice_fusion
  37.4 0.7 broadcast_multiply_fusion
  38.1 0.8 dynamic-slice_compare_fusion
  38.8 0.7 convert_element_type.64
  39.5 0.8 slice.100
  40.3 0.1 dynamic_slice.29
  40.4 0.2 select_reduce_fusion.1
  40.6 0.1 fusion.46
  40.7 0.1 fusion.10
  40.8 0.1 bitcast_select_fusion
  40.9 10.0 %all-to-all-done = bf16[32,32,128]{2,1,0:T(8,128)(2,1)S(1)} async-done(((bf16[32,32,128]{2,1,0:T(8,128)(2,1)}), bf16[32,32,128]{2,1,0:T(8,128)(2,1)S(1)}, u32[]{:S(2)}, u32[]{:S(2)}) %all-to-all-start) | async-done | bytes 262176 | tf_op jit(solution)/shard_map/all_to_all | solution.py:251
  50.9 0.1 concatenate.31
  51.0 0.1 concatenate.32
  51.1 0.1 fusion.44
  51.2 0.7 broadcast_in_dim.87
  51.8 4.9 %all-to-all-start.1 = ((bf16[16,32,128]{2,1,0:T(8,128)(2,1)}), bf16[16,32,128]{2,1,0:T(8,128)(2,1)S(1)}, u32[]{:S(2)}, u32[]{:S(2)}) async-start(bf16[16,32,128]{2,1,0:T(8,128)(2,1)} %broadcast_in_dim.87), calls=%async_computation.1 | async-start | bytes 262144 | tf_op jit(solution)/shard_map/all_to_all | solution.py:21
  56.8 0.9 select_reduce_fusion
  57.7 0.1 dynamic-slice_bitcast_fusion
  57.8 0.0 collective-permute-done.1
  57.8 0.9 fusion.11
  58.7 0.0 collective-permute-done.far_ref
  58.7 10.1 %all-to-all-done.1.rows_ref = bf16[16,32,128]{2,1,0:T(8,128)(2,1)S(1)} async-done(((bf16[16,32,128]{2,1,0:T(8,128)(2,1)}), bf16[16,32,128]{2,1,0:T(8,128)(2,1)S(1)}, u32[]{:S(2)}, u32[]{:S(2)}) %all-to-all-start.1) | async-done | bytes 131104 | tf_op jit(solution)/shard_map/all_to_all | solution.py:21
  68.8 1.6 second_terms.1
  70.4 9.2 %all_to_all.70 = s16[8,8,640]{2,1,0:T(8,128)(2,1)S(1)} all-to-all(s16[8,8,640]{2,1,0:T(8,128)(2,1)S(1)} %convert_element_type.69), channel_id=1, replica_groups=mesh['xh'=2,'core'=2,'xl'=2,'z'=16,'y'=4] {'xl','y'}, dimensions={0} | all-to-all | bytes 163840 | tf_op jit(solution)/shard_map/all_to_all | solution.py:302
  79.7 0.1 reshape.185
  79.8 0.1 negate_select_fusion.8
  79.9 17.7 %all_to_all.71 = bf16[16,8,512]{2,1,0:T(8,128)(2,1)S(1)} all-to-all(bf16[16,8,512]{2,1,0:T(8,128)(2,1)S(1)} %broadcast_in_dim.161), channel_id=1, replica_groups=mesh['xh'=2,'core'=2,'xl'=2,'z'=16,'y'=4] {'z'}, dimensions={0} | all-to-all | bytes 262144 | tf_op jit(solution)/shard_map/all_to_all | solution.py:21
  97.6 0.0 all-gather.3.cloned.1.call-done
  97.6 3.5 %in_spin_order.1 = bf16[16,8,64,512]{3,2,1,0:T(8,128)(2,1)S(1)} custom-call(bf16[2,2,4,16,64,256]{5,4,3,2,1,0:T(8,128)(2,1)} %bitcast.97), custom_call_target="tpu_custom_call" | custom-call | tf_op jit(solution)/shard_map/in_spin_order/pallas_call | solution.py:46
  101.1 1.2 fusion.7
  102.3 15.9 %all_to_all.72 = bf16[16,8,512]{2,1,0:T(8,128)(2,1)S(1)} all-to-all(bf16[16,8,512]{2,1,0:T(8,128)(2,1)S(1)} %broadcast_in_dim.162), channel_id=1, replica_groups=mesh['xh'=2,'core'=2,'xl'=2,'z'=16,'y'=4] {'z'}, dimensions={0} | all-to-all | bytes 262144 | tf_op jit(solution)/shard_map/all_to_all | solution.py:21
  118.2 1.1 fusion.6
  119.4 15.8 %all_to_all.73 = bf16[16,8,512]{2,1,0:T(8,128)(2,1)S(1)} all-to-all(bf16[16,8,512]{2,1,0:T(8,128)(2,1)S(1)} %broadcast_in_dim.163), channel_id=1, replica_groups=mesh['xh'=2,'core'=2,'xl'=2,'z'=16,'y'=4] {'z'}, dimensions={0} | all-to-all | bytes 262144 | tf_op jit(solution)/shard_map/all_to_all | solution.py:21
  135.2 1.1 fusion.5
  136.4 15.8 %all_to_all.74 = bf16[16,8,512]{2,1,0:T(8,128)(2,1)S(1)} all-to-all(bf16[16,8,512]{2,1,0:T(8,128)(2,1)S(1)} %broadcast_in_dim.164), channel_id=1, replica_groups=mesh['xh'=2,'core'=2,'xl'=2,'z'=16,'y'=4] {'z'}, dimensions={0} | all-to-all | bytes 262144 | tf_op jit(solution)/shard_map/all_to_all | solution.py:21
  152.3 1.1 fusion.4
  153.5 15.8 %all_to_all.75 = bf16[16,8,512]{2,1,0:T(8,128)(2,1)S(1)} all-to-all(bf16[16,8,512]{2,1,0:T(8,128)(2,1)S(1)} %broadcast_in_dim.165), channel_id=1, replica_groups=mesh['xh'=2,'core'=2,'xl'=2,'z'=16,'y'=4] {'z'}, dimensions={0} | all-to-all | bytes 262144 | tf_op jit(solution)/shard_map/all_to_all | solution.py:21
  169.2 1.1 fusion.3
  170.5 15.6 %all_to_all.76 = bf16[16,8,512]{2,1,0:T(8,128)(2,1)S(1)} all-to-all(bf16[16,8,512]{2,1,0:T(8,128)(2,1)S(1)} %broadcast_in_dim.166), channel_id=1, replica_groups=mesh['xh'=2,'core'=2,'xl'=2,'z'=16,'y'=4] {'z'}, dimensions={0} | all-to-all | bytes 262144 | tf_op jit(solution)/shard_map/all_to_all | solution.py:21
  186.1 1.1 fusion.2
  187.3 15.4 %all_to_all.77 = bf16[16,8,512]{2,1,0:T(8,128)(2,1)S(1)} all-to-all(bf16[16,8,512]{2,1,0:T(8,128)(2,1)S(1)} %broadcast_in_dim.167), channel_id=1, replica_groups=mesh['xh'=2,'core'=2,'xl'=2,'z'=16,'y'=4] {'z'}, dimensions={0} | all-to-all | bytes 262144 | tf_op jit(solution)/shard_map/all_to_all | solution.py:21
  202.8 1.1 fusion.1
  204.0 15.6 %all_to_all.78 = bf16[16,8,512]{2,1,0:T(8,128)(2,1)S(1)} all-to-all(bf16[16,8,512]{2,1,0:T(8,128)(2,1)S(1)} %broadcast_in_dim.168), channel_id=1, replica_groups=mesh['xh'=2,'core'=2,'xl'=2,'z'=16,'y'=4] {'z'}, dimensions={0} | all-to-all | bytes 262144 | tf_op jit(solution)/shard_map/all_to_all | solution.py:21
  219.6 1.1 fusion
  220.9 15.5 %all_to_all.79 = bf16[16,8,512]{2,1,0:T(8,128)(2,1)S(1)} all-to-all(bf16[16,8,512]{2,1,0:T(8,128)(2,1)S(1)} %broadcast_in_dim.169), channel_id=1, replica_groups=mesh['xh'=2,'core'=2,'xl'=2,'z'=16,'y'=4] {'z'}, dimensions={0} | all-to-all | bytes 262144 | tf_op jit(solution)/shard_map/all_to_all | solution.py:21
  236.4 1.3 fusion.8
  237.7 14.9 %all_to_all.80 = f32[16,1,128]{2,1,0:T(1,128)S(1)} all-to-all(f32[16,1,128]{2,1,0:T(1,128)S(1)} %broadcast_in_dim.170), channel_id=1, replica_groups=mesh['xh'=2,'core'=2,'xl'=2,'z'=16,'y'=4] {'z'}, dimensions={0} | all-to-all | bytes 16384 | tf_op jit(solution)/shard_map/all_to_all | solution.py:21
  252.6 0.1 last_blocks.1
  252.7 29.3 %all_to_all.81 = bf16[32,8,384]{2,1,0:T(8,128)(2,1)S(1)} all-to-all(bf16[32,8,384]{2,1,0:T(8,128)(2,1)S(1)} %last_blocks.1), channel_id=1, replica_groups=mesh['xh'=2,'core'=2,'xl'=2,'z'=16,'y'=4] {'xh','core','xl','y'}, dimensions={0} | all-to-all | bytes 393216 | tf_op jit(solution)/shard_map/all_to_all | solution.py:337
  282.0 0.2 fusion.41
  282.2 0.2 fusion.14
  282.4 0.2 fusion.16
  282.5 0.5 select_multiply_fusion
  283.1 0.7 fusion.9
  (40 shorter events, 0.7 us)
Async XLA Ops:
  7.2 90.4 %all-gather.3.cloned.1.call-start = ((), (), s32[]{:S(2)}) async-start(), calls=%async_computation.14 | async-start | bytes 8912896 | tf_op jit(solution)/shard_map/all_gather | solution.py:250
  12.0 45.8 %collective-permute-start.1 = (f32[9,8,256]{2,1,0:T(8,128)S(1)}, f32[9,8,256]{2,1,0:T(8,128)S(1)}, u32[]{:S(2)}, u32[]{:S(2)}) collective-permute-start(f32[9,8,256]{2,1,0:T(8,128)S(1)} %dynamic-slice_select_fusion), channel_id=1, source_target_pairs={{0,64},{64,0},{1,65},{65,1},{2,66},{66,2},{3,67},{67,3},{4,68},{68... | collective-permute-start | bytes 221192 | tf_op jit(solution)/shard_map/ppermute | solution.py:290
  15.9 35.0 %all-to-all-start = ((bf16[32,32,128]{2,1,0:T(8,128)(2,1)}), bf16[32,32,128]{2,1,0:T(8,128)(2,1)S(1)}, u32[]{:S(2)}, u32[]{:S(2)}) async-start(bf16[32,32,128]{2,1,0:T(8,128)(2,1)} %get-tuple-element.21), calls=%async_computation | async-start | bytes 524288 | tf_op jit(solution)/shard_map/all_to_all | solution.py:251
  31.1 27.6 %collective-permute-start = (bf16[1024,256]{1,0:T(8,128)(2,1)S(1)}, bf16[1024,256]{1,0:T(8,128)(2,1)S(1)}, u32[]{:S(2)}, u32[]{:S(2)}) collective-permute-start(bf16[1024,256]{1,0:T(8,128)(2,1)S(1)} %get-tuple-element.22), channel_id=1, source_target_pairs={{0,320},{320,0},{64,256},{256,64},{1,321},{321,1},{65,257},{257,65... | collective-permute-start | bytes 1572872 | tf_op jit(solution)/shard_map/ppermute | solution.py:252
  51.8 16.9 %all-to-all-start.1 = ((bf16[16,32,128]{2,1,0:T(8,128)(2,1)}), bf16[16,32,128]{2,1,0:T(8,128)(2,1)S(1)}, u32[]{:S(2)}, u32[]{:S(2)}) async-start(bf16[16,32,128]{2,1,0:T(8,128)(2,1)} %broadcast_in_dim.87), calls=%async_computation.1 | async-start | bytes 262144 | tf_op jit(solution)/shard_map/all_to_all | solution.py:21
Sparse Core Ops, SparseCore 0:
  10.4 68.0 all-gather.2
